TPU v7x, 32 devices: a whole 2x2x4 slice. The times are simulated.
32 devices in a mesh: segment: 4 (over x, core), dp: 8 (over z, y).
Axes of the slice: x: 2, y: 2, z: 4, core: 2. Of those that a mesh axis runs over, the one named last changes fastest.
Arguments:
- embeds: bfloat16 [2, 8, 128, 4096], P(None, 'dp'), may hold values from -6 to 6
- base_weight: bfloat16 [4, 4096, 4096], P('segment', 'dp'), may hold values from -0.09375 to 0.09375
- norm_gain: float32 [4, 4096], P('segment'), may hold values from 0.25 to 1.75
- skill_down: bfloat16 [4, 16, 8, 4096], P('segment'), may hold values from -0.09375 to 0.09375
- skill_up: bfloat16 [4, 16, 8, 4096], P('segment'), may hold values from -2 to 2
- task_ids: int32 [2, 8], replicated, may hold values from 0 to 1835
- allocation: int32 [1836, 16], replicated, may hold values 0 or 1
- target_lengths: int32 [2, 8], replicated, may hold values from 1 to 128
- cotangent: bfloat16 [2, 8, 128, 4096], P(None, 'dp'), may hold values from -6 to 6
Outputs:
- hidden: bfloat16 [4, 2, 8, 128, 4096], P('segment', None, 'dp')
- input_grads: bfloat16 [4, 2, 8, 128, 4096], P('segment', None, 'dp')
- grad_down: float32 [4, 16, 8, 4096], P('segment', None, None, 'dp')
- grad_up: float32 [4, 16, 8, 4096], P('segment', None, None, 'dp')
All inputs are finite; a program needn't handle non-finite values.
Results may differ from a plain program's by a relative error of at most 0.019.
Values may be sent and summed in bfloat16 or wider, within the bound.
No kernel may reach another device: no remote copies, remote signals or barrier semaphores. Data moves between devices by JAX's collectives and lax.ppermute only.
A program may use at most 192 MiB of HBM per device.

v0:
```python
import jax
import jax.numpy as jnp
from jax import lax
from jax.sharding import PartitionSpec as P

EPS = 1e-06


def shifted(block, axis, distance):
    devices = range(lax.axis_size(axis))
    route = [(i - distance, i) for i in devices if i - distance in devices]
    return lax.ppermute(block, axis, route)


def prepare(x, gain, down_t):
    xf = x.astype(jnp.float32)
    inv = lax.rsqrt(jnp.mean(xf * xf, axis=-1, keepdims=True) + EPS)
    normed = (xf * inv * gain).astype(jnp.bfloat16)
    low = jnp.dot(normed, down_t.T, preferred_element_type=jnp.float32).astype(jnp.bfloat16)
    return (normed, low, inv)


def forward_full(x, weight, gain, down_t, up_t):
    normed, low, inv = prepare(x, gain, down_t)
    total = x.astype(jnp.float32) + jnp.dot(normed, weight, preferred_element_type=jnp.float32)
    total = total + jnp.dot(low, up_t, preferred_element_type=jnp.float32)
    return (total.astype(jnp.bfloat16), normed, low, inv)


def backward_core(x, normed, low, inv, grad_out, weight, gain, down_t, up_t):
    g_low = jnp.dot(grad_out, up_t.T, preferred_element_type=jnp.float32).astype(jnp.bfloat16)
    dnorm = jnp.dot(grad_out, weight.T, preferred_element_type=jnp.float32)
    dnorm = dnorm + jnp.dot(g_low, down_t, preferred_element_type=jnp.float32)
    seq_down = jnp.dot(g_low.T, normed, preferred_element_type=jnp.float32)
    seq_up = jnp.dot(low.T, grad_out, preferred_element_type=jnp.float32)
    xf = x.astype(jnp.float32)
    scaled = gain * dnorm
    grad_in = (
        grad_out.astype(jnp.float32)
        + inv * scaled
        - xf * inv * inv * inv * jnp.mean(xf * scaled, axis=-1, keepdims=True)
    )
    return (grad_in.astype(jnp.bfloat16), seq_down, seq_up)


def pick(table, index):
    return lax.dynamic_index_in_dim(table, index, 0, keepdims=False)


def place(table, value, index, active):
    return jnp.where(active, lax.dynamic_update_index_in_dim(table, value, index, 0), table)


def shards(
    embeds,
    base_weight,
    norm_gain,
    skill_down,
    skill_up,
    task_ids,
    allocation,
    target_lengths,
    cotangent,
):
    segments = lax.axis_size("segment")
    segment = lax.axis_index("segment")
    member = lax.axis_index("dp")
    weight = lax.all_gather(base_weight[0], "dp", axis=0, tiled=True)
    gain = norm_gain[0]
    micro = embeds.shape[0]
    rows = embeds.shape[2]
    width = embeds.shape[3]
    splits = 1
    blocks = micro * splits
    block_rows = rows // splits
    tasks = lax.dynamic_index_in_dim(task_ids, member, 1, keepdims=False)
    lengths = lax.dynamic_index_in_dim(target_lengths, member, 1, keepdims=False)
    onehot = (tasks[:, None] == jnp.arange(allocation.shape[0], dtype=jnp.int32)[None, :]).astype(
        jnp.float32
    )
    alloc = allocation.astype(jnp.float32)
    counts = jnp.maximum(jnp.sum(alloc, axis=1, keepdims=True), 1.0)
    mix = jnp.einsum("mt,ts->ms", onehot, alloc / counts, precision=lax.Precision.HIGHEST)
    down_seq = jnp.einsum(
        "ms,srd->mrd", mix, skill_down[0].astype(jnp.float32), precision=lax.Precision.HIGHEST
    ).astype(jnp.bfloat16)
    up_seq = jnp.einsum(
        "ms,srd->mrd", mix, skill_up[0].astype(jnp.float32), precision=lax.Precision.HIGHEST
    ).astype(jnp.bfloat16)
    down_all = jnp.repeat(down_seq, splits, axis=0)
    up_all = jnp.repeat(up_seq, splits, axis=0)
    mix_all = jnp.repeat(mix, splits, axis=0)
    firsts = embeds[:, 0]
    live = jnp.arange(rows, dtype=jnp.int32)[None, :] < lengths[:, None]
    seeds = cotangent[:, 0] * live[..., None].astype(jnp.bfloat16)
    ticks = segments + blocks - 1
    rank = down_all.shape[1]
    blank = jnp.zeros((block_rows, width), jnp.bfloat16)
    stack_blank = jnp.zeros((blocks, block_rows, width), jnp.bfloat16)
    low_blank = jnp.zeros((blocks, block_rows, rank), jnp.bfloat16)
    inv_blank = jnp.zeros((blocks, block_rows, 1), jnp.float32)

    def forward_tick(tick, carry):
        incoming, saved, outs, kept_norm, kept_low, kept_inv = carry
        slot = tick - segment
        active = (slot >= 0) & (slot < blocks)
        index = jnp.clip(slot, 0, blocks - 1)
        x = jnp.where(segment == 0, pick(firsts, index), incoming)
        result, normed, low, inv = lax.cond(
            active,
            lambda: forward_full(x, weight, gain, pick(down_all, index), pick(up_all, index)),
            lambda: (
                blank,
                blank,
                jnp.zeros((block_rows, rank), jnp.bfloat16),
                jnp.zeros((block_rows, 1), jnp.float32),
            ),
        )
        saved = place(saved, x, index, active)
        outs = place(outs, result, index, active)
        return (result, (saved, outs, kept_norm, kept_low, kept_inv))

    def forward_step(tick, carry):
        result, rest = forward_tick(tick, carry)
        moved = shifted(result, "segment", 1)
        return (moved,) + rest

    carry = (blank, stack_blank, stack_blank, stack_blank, low_blank, inv_blank)
    carry = lax.fori_loop(0, ticks - 1, forward_step, carry)
    _, (saved, outs, kept_norm, kept_low, kept_inv) = forward_tick(ticks - 1, carry)
    skills = skill_down.shape[1]
    acc_blank = jnp.zeros((skills, rank, width), jnp.float32)

    def backward_tick(tick, carry):
        incoming, grads_in, acc_down, acc_up = carry
        slot = tick - (segments - 1 - segment)
        active = (slot >= 0) & (slot < blocks)
        index = jnp.clip(slot, 0, blocks - 1)
        grad_out = jnp.where(segment == segments - 1, pick(seeds, index), incoming)
        x = pick(saved, index)
        down_t = pick(down_all, index)
        up_t = pick(up_all, index)

        def run():
            normed, low, inv = prepare(x, gain, down_t)
            return backward_core(x, normed, low, inv, grad_out, weight, gain, down_t, up_t)

        grad_in, seq_down, seq_up = lax.cond(
            active,
            run,
            lambda: (
                blank,
                jnp.zeros((rank, width), jnp.float32),
                jnp.zeros((rank, width), jnp.float32),
            ),
        )
        weights = pick(mix_all, index)[:, None, None]
        acc_down = acc_down + weights * seq_down[None]
        acc_up = acc_up + weights * seq_up[None]
        grads_in = place(grads_in, grad_in, index, active)
        return (grad_in, (grads_in, acc_down, acc_up))

    def backward_step(tick, carry):
        grad_in, rest = backward_tick(tick, carry)
        moved = shifted(grad_in, "segment", -1)
        return (moved,) + rest

    carry = (blank, stack_blank, acc_blank, acc_blank)
    carry = lax.fori_loop(0, ticks - 1, backward_step, carry)
    _, (grads_in, acc_down, acc_up) = backward_tick(ticks - 1, carry)
    grad_down, grad_up = (
        lax.psum_scatter(
            acc_down.astype(jnp.bfloat16), "dp", scatter_dimension=2, tiled=True
        ).astype(jnp.float32),
        lax.psum_scatter(acc_up.astype(jnp.bfloat16), "dp", scatter_dimension=2, tiled=True).astype(
            jnp.float32
        ),
    )
    return (outs[None, :, None], grads_in[None, :, None], grad_down[None], grad_up[None])


def solution(mesh):
    in_specs = (
        P(None, "dp", None, None),
        P("segment", "dp", None),
        P("segment", None),
        P("segment", None, None, None),
        P("segment", None, None, None),
        P(),
        P(),
        P(),
        P(None, "dp", None, None),
    )
    out_specs = (
        P("segment", None, "dp", None, None),
        P("segment", None, "dp", None, None),
        P("segment", None, None, "dp"),
        P("segment", None, None, "dp"),
    )
    return jax.shard_map(shards, mesh=mesh, in_specs=in_specs, out_specs=out_specs, check_vma=False)
```

profile of v0, /device:TPU:0, one launch (start us, length us, event | category | flops | bytes accessed | tf_op | source)
XLA Modules:
  0.0 1101.7 jit_solution(8175166725081357591)
XLA Ops:
  16.1 633.9 %all-gather.3.cloned.1.call-done = bf16[1,4096,4096]{2,1,0:T(8,128)(2,1)} async-done(((bf16[1,512,4096]{2,1,0:T(8,128)(2,1)}), bf16[1,4096,4096]{2,1,0:T(8,128)(2,1)}) %all-gather.3.cloned.1.call-update) | async-done | bytes 33554448 | tf_op jit(solution)/shard_map/all_gather | solution.py:68
  652.9 111.1 %while.40 = (s32[]{:T(128)}, bf16[128,4096]{1,0:T(8,128)(2,1)}, bf16[2,128,4096]{2,1,0:T(8,128)(2,1)S(1)}, bf16[2,128,4096]{2,1,0:T(8,128)(2,1)}, s32[]{:T(128)}...) while((s32[]{:T(128)}, bf16[128,4096]{1,0:T(8,128)(2,1)}, ...), condition=%wide.region_5.6_spmd, body=%wide.region_1.5_spmd.sunk | while | flops 4321182720 | bytes 77762976 | solution.py:129
  656.1 18.8 %conditional.9 = (bf16[128,4096]{1,0:T(8,128)(2,1)S(1)}, bf16[1,128,4096]{2,1,0:T(8,128)(2,1)}) conditional(s32[]{:T(128)} %convert_element_type.342, () %tuple.144, (bf16[128,4096]{1,0:T(8,128)(2,1)S(1)}, f32[1,4096]{1,0:T(1,128)S(1)}, bf16[4096,4096]{1,0:T(8,128)(2,1)}, s32[]{:T(128)}, bf16[2,8,4096]{2,1,0:T(8,128)(2,1)S(1)}, ...), branch_computations={%region_2.2_spmd, %region_3.4_spmd} | conditional | flops 4319609856 | bytes 48401996 | solution.py:109
  656.4 13.0 %convolution_add_fusion.1 = f32[128,4096]{1,0:T(8,128)S(1)} fusion(bf16[4096,4096]{1,0:T(8,128)(2,1)} %get-tuple-element.684, bf16[128,4096]{1,0:T(8,128)(2,1)S(1)} %get-tuple-element.682, f32[4096]{0:T(1024)S(1)} %bitcast.180, f32[128]{0:T(128)S(1)} %add_rsqrt_fusion), kind=kOutput, calls=%fused_computation.1 | convolution fusion | flops 4298113024 | bytes 36717056 | tf_op jit(solution)/shard_map/while/body/eval_jaxpr/cond/branch_1_fun/dot_general | solution.py:25
  683.3 18.8 %conditional.9 = (bf16[128,4096]{1,0:T(8,128)(2,1)S(1)}, bf16[1,128,4096]{2,1,0:T(8,128)(2,1)}) conditional(s32[]{:T(128)} %convert_element_type.342, () %tuple.144, (bf16[128,4096]{1,0:T(8,128)(2,1)S(1)}, f32[1,4096]{1,0:T(1,128)S(1)}, bf16[4096,4096]{1,0:T(8,128)(2,1)}, s32[]{:T(128)}, bf16[2,8,4096]{2,1,0:T(8,128)(2,1)S(1)}, ...), branch_computations={%region_2.2_spmd, %region_3.4_spmd} | conditional | flops 4319609856 | bytes 48401996 | solution.py:109
  683.6 13.0 %convolution_add_fusion.1 = f32[128,4096]{1,0:T(8,128)S(1)} fusion(bf16[4096,4096]{1,0:T(8,128)(2,1)} %get-tuple-element.684, bf16[128,4096]{1,0:T(8,128)(2,1)S(1)} %get-tuple-element.682, f32[4096]{0:T(1024)S(1)} %bitcast.180, f32[128]{0:T(128)S(1)} %add_rsqrt_fusion), kind=kOutput, calls=%fused_computation.1 | convolution fusion | flops 4298113024 | bytes 36717056 | tf_op jit(solution)/shard_map/while/body/eval_jaxpr/cond/branch_1_fun/dot_general | solution.py:25
  711.7 28.8 %collective-permute-start = (bf16[128,4096]{1,0:T(8,128)(2,1)S(1)}, bf16[128,4096]{1,0:T(8,128)(2,1)}, u32[]{:S(2)}, u32[]{:S(2)}) collective-permute-start(bf16[128,4096]{1,0:T(8,128)(2,1)S(1)} %get-tuple-element.1077), channel_id=1, source_target_pairs={{0,8},{8,16},{16,24},{1,9},{9,17},{17,25},{2,10},{10,18},{18,26},{... | collective-permute-start | bytes 3145736 | tf_op jit(solution)/shard_map/while/body/eval_jaxpr/ppermute | solution.py:12
  747.3 14.2 %collective-permute-start = (bf16[128,4096]{1,0:T(8,128)(2,1)S(1)}, bf16[128,4096]{1,0:T(8,128)(2,1)}, u32[]{:S(2)}, u32[]{:S(2)}) collective-permute-start(bf16[128,4096]{1,0:T(8,128)(2,1)S(1)} %get-tuple-element.1077), channel_id=1, source_target_pairs={{0,8},{8,16},{16,24},{1,9},{9,17},{17,25},{2,10},{10,18},{18,26},{... | collective-permute-start | bytes 3145736 | tf_op jit(solution)/shard_map/while/body/eval_jaxpr/ppermute | solution.py:12
  769.5 166.3 %while.41 = (s32[]{:T(128)}, bf16[128,4096]{1,0:T(8,128)(2,1)}, bf16[2,128,4096]{2,1,0:T(8,128)(2,1)}, f32[16,8,4096]{2,1,0:T(8,128)}, f32[16,8,4096]{2,1,0:T(8,...) while((s32[]{:T(128)}, bf16[128,4096]{1,0:T(8,128)(2,1)}, ...), condition=%wide.region_14.15_spmd.clone, body=%wide.region_9.14_spmd.clone.sunk | while | flops 4354214400 | bytes 94118616 | solution.py:169
  779.1 25.7 %collective-permute-done.1 = bf16[128,4096]{1,0:T(8,128)(2,1)S(1)} collective-permute-done((bf16[128,4096]{1,0:T(8,128)(2,1)}, bf16[128,4096]{1,0:T(8,128)(2,1)S(1)}, u32[]{:S(2)}, u32[]{:S(2)}) %collective-permute-start.1) | collective-permute-done | bytes 1048608 | tf_op jit(solution)/shard_map/while/body/eval_jaxpr/ppermute | solution.py:12
  812.7 4.4 select_add_fusion.3
  817.0 8.2 collective-permute-done.1
  833.1 4.4 select_add_fusion.3
  837.5 53.9 %collective-permute-done.1 = bf16[128,4096]{1,0:T(8,128)(2,1)S(1)} collective-permute-done((bf16[128,4096]{1,0:T(8,128)(2,1)}, bf16[128,4096]{1,0:T(8,128)(2,1)S(1)}, u32[]{:S(2)}, u32[]{:S(2)}) %collective-permute-start.1) | collective-permute-done | bytes 1048608 | tf_op jit(solution)/shard_map/while/body/eval_jaxpr/ppermute | solution.py:12
  892.5 25.9 %conditional.10 = (bf16[128,4096]{1,0:T(8,128)(2,1)}, f32[8,4096]{1,0:T(8,128)S(1)}, f32[8,4096]{1,0:T(8,128)S(1)}, bf16[1,128,4096]{2,1,0:T(8,128)(2,1)}) conditional(s32[]{:T(128)} %convert_element_type.343, () %tuple.148, (pred[]{:T(512)}, bf16[2,128,4096]{2,1,0:T(8,128)(2,1)}, s32[]{:T(128)}, bf16[128,4096]{1,0:T(8,128)(2,1)}, ...), branch_computations={%region_10.10_spmd, %region_11.13_spmd} | conditional | flops 4350544384 | bytes 57155172 | solution.py:148
  895.4 16.0 %fusion.153 = f32[128,4096]{1,0:T(8,128)S(1)} fusion(bf16[128,4096]{1,0:T(8,128)(2,1)S(1)} %bitcast_select_fusion.2, bf16[4096,4096]{1,0:T(8,128)(2,1)} %get-tuple-element.714), kind=kOutput, calls=%fused_computation.166 | convolution fusion | flops 4294967296 | bytes 36700160 | tf_op jit(solution)/shard_map/while/body/eval_jaxpr/cond/branch_1_fun/dot_general | solution.py:32
  923.3 4.4 select_add_fusion.3
  927.7 7.0 collective-permute-done.1
  935.8 22.5 %conditional.5 = (f32[8,4096]{1,0:T(8,128)S(1)}, f32[8,4096]{1,0:T(8,128)S(1)}, bf16[1,128,4096]{2,1,0:T(8,128)(2,1)}) conditional(s32[]{:T(128)} %convert_element_type.170, () %tuple.98, (pred[]{:T(512)}, bf16[2,128,4096]{2,1,0:T(8,128)(2,1)}, s32[]{:T(128)}, bf16[128,4096]{1,0:T(8,128)(2,1)}, bf16[2,8,4096]{2,0,1:T(2,128)(2,1)}, ...), branch_computations={%region_15.16_spmd, %region_16.19_spmd} | conditional | flops 4350544384 | bytes 56620128 | solution.py:148
  937.9 16.0 %fusion.154 = f32[128,4096]{1,0:T(8,128)S(1)} fusion(bf16[128,4096]{1,0:T(8,128)(2,1)S(1)} %bitcast_select_fusion.3, bf16[4096,4096]{1,0:T(8,128)(2,1)} %get-tuple-element.744), kind=kOutput, calls=%fused_computation.167 | convolution fusion | flops 4294967296 | bytes 36700160 | tf_op jit(solution)/shard_map/cond/branch_1_fun/dot_general | solution.py:32
  958.3 4.2 add_convert_fusion
  969.1 3.7 bitcast_dynamic-update-slice_fusion
  972.9 53.5 %reduce-scatter.5.cloned.1.call-done = bf16[16,8,512]{2,1,0:T(8,128)(2,1)} async-done(((bf16[16,8,4096]{2,1,0:T(8,128)(2,1)}), bf16[16,8,512]{2,1,0:T(8,128)(2,1)}) %reduce-scatter.5.cloned.1.call-update) | async-done | bytes 131088 | tf_op jit(solution)/shard_map/reduce_scatter | solution.py:175
  1028.0 65.5 %reduce-scatter.3.cloned.1.call-done = bf16[16,8,512]{2,1,0:T(8,128)(2,1)} async-done(((bf16[16,8,4096]{2,1,0:T(8,128)(2,1)}), bf16[16,8,512]{2,1,0:T(8,128)(2,1)}) %reduce-scatter.3.cloned.1.call-update) | async-done | bytes 131088 | tf_op jit(solution)/shard_map/reduce_scatter | solution.py:172
  (187 shorter events, 127.5 us)
Async XLA Ops:
  7.2 642.8 %all-gather.3.cloned.1.call-start = ((), (), s32[]{:S(2)}) async-start(), calls=%async_computation.4 | async-start | bytes 37748736 | tf_op jit(solution)/shard_map/all_gather | solution.py:68
  7.9 5.8 copy-start.25
  7.9 6.6 copy-start.12
  8.0 1018.4 %reduce-scatter.5.cloned.1.call-start = ((), (), s32[]{:S(2)}) async-start(), calls=%async_computation.3 | async-start | bytes 1179648 | tf_op jit(solution)/shard_map/reduce_scatter | solution.py:175
  8.5 7.6 copy-start.23
  10.1 6.0 copy-start.13
  674.9 5.3 collective-permute-start
  702.2 5.2 collective-permute-start
  711.7 31.3 %copy-start.3 = (bf16[2,128,4096]{2,1,0:T(8,128)(2,1)S(1)}, bf16[2,128,4096]{2,1,0:T(8,128)(2,1)}, u32[]{:S(2)}) copy-start(bf16[2,128,4096]{2,1,0:T(8,128)(2,1)} %copy-done.2) | copy-start | bytes 6291460 | tf_op jit(solution)/shard_map/while
  711.7 31.3 %collective-permute-start = (bf16[128,4096]{1,0:T(8,128)(2,1)S(1)}, bf16[128,4096]{1,0:T(8,128)(2,1)}, u32[]{:S(2)}, u32[]{:S(2)}) collective-permute-start(bf16[128,4096]{1,0:T(8,128)(2,1)S(1)} %get-tuple-element.1077), channel_id=1, source_target_pairs={{0,8},{8,16},{16,24},{1,9},{9,17},{17,25},{2,10},{10,18},{18,26},{... | collective-permute-start | bytes 3145736 | tf_op jit(solution)/shard_map/while/body/eval_jaxpr/ppermute | solution.py:12
  747.3 16.7 %copy-start.3 = (bf16[2,128,4096]{2,1,0:T(8,128)(2,1)S(1)}, bf16[2,128,4096]{2,1,0:T(8,128)(2,1)}, u32[]{:S(2)}) copy-start(bf16[2,128,4096]{2,1,0:T(8,128)(2,1)} %copy-done.2) | copy-start | bytes 6291460 | tf_op jit(solution)/shard_map/while
  747.3 16.7 %collective-permute-start = (bf16[128,4096]{1,0:T(8,128)(2,1)S(1)}, bf16[128,4096]{1,0:T(8,128)(2,1)}, u32[]{:S(2)}, u32[]{:S(2)}) collective-permute-start(bf16[128,4096]{1,0:T(8,128)(2,1)S(1)} %get-tuple-element.1077), channel_id=1, source_target_pairs={{0,8},{8,16},{16,24},{1,9},{9,17},{17,25},{2,10},{10,18},{18,26},{... | collective-permute-start | bytes 3145736 | tf_op jit(solution)/shard_map/while/body/eval_jaxpr/ppermute | solution.py:12
  771.7 33.0 %collective-permute-start.1 = (bf16[128,4096]{1,0:T(8,128)(2,1)}, bf16[128,4096]{1,0:T(8,128)(2,1)S(1)}, u32[]{:S(2)}, u32[]{:S(2)}) collective-permute-start(bf16[128,4096]{1,0:T(8,128)(2,1)} %get-tuple-element.1094), channel_id=1, source_target_pairs={{8,0},{16,8},{24,16},{9,1},{17,9},{25,17},{10,2},{18,10},{26,18},{... | collective-permute-start | bytes 3145736 | tf_op jit(solution)/shard_map/while/body/eval_jaxpr/ppermute | solution.py:12
  779.1 25.7 %copy-start.6 = (f32[16,8,4096]{2,1,0:T(8,128)}, f32[16,8,4096]{2,1,0:T(8,128)S(1)}, u32[]{:S(2)}) copy-start(f32[16,8,4096]{2,1,0:T(8,128)S(1)} %get-tuple-element.1191) | copy-start | bytes 6291460 | tf_op jit(solution)/shard_map/while
  808.1 17.2 %collective-permute-start.1 = (bf16[128,4096]{1,0:T(8,128)(2,1)}, bf16[128,4096]{1,0:T(8,128)(2,1)S(1)}, u32[]{:S(2)}, u32[]{:S(2)}) collective-permute-start(bf16[128,4096]{1,0:T(8,128)(2,1)} %get-tuple-element.1094), channel_id=1, source_target_pairs={{8,0},{16,8},{24,16},{9,1},{17,9},{25,17},{10,2},{18,10},{26,18},{... | collective-permute-start | bytes 3145736 | tf_op jit(solution)/shard_map/while/body/eval_jaxpr/ppermute | solution.py:12
  817.0 8.2 copy-start.6
  828.5 62.9 %collective-permute-start.1 = (bf16[128,4096]{1,0:T(8,128)(2,1)}, bf16[128,4096]{1,0:T(8,128)(2,1)S(1)}, u32[]{:S(2)}, u32[]{:S(2)}) collective-permute-start(bf16[128,4096]{1,0:T(8,128)(2,1)} %get-tuple-element.1094), channel_id=1, source_target_pairs={{8,0},{16,8},{24,16},{9,1},{17,9},{25,17},{10,2},{18,10},{26,18},{... | collective-permute-start | bytes 3145736 | tf_op jit(solution)/shard_map/while/body/eval_jaxpr/ppermute | solution.py:12
  837.5 53.9 %copy-start.6 = (f32[16,8,4096]{2,1,0:T(8,128)}, f32[16,8,4096]{2,1,0:T(8,128)S(1)}, u32[]{:S(2)}) copy-start(f32[16,8,4096]{2,1,0:T(8,128)S(1)} %get-tuple-element.1191) | copy-start | bytes 6291460 | tf_op jit(solution)/shard_map/while
  895.3 16.0 %copy-start.19 = (bf16[128,8]{0,1:T(8,128)(2,1)}, bf16[128,8]{0,1:T(8,128)(2,1)S(1)}, u32[]{:S(2)}) copy-start(bf16[128,8]{0,1:T(8,128)(2,1)S(1)} %convolution_convert_fusion.1) | copy-start | bytes 6148 | tf_op jit(solution)/shard_map/while/body/eval_jaxpr/cond
  918.4 16.3 %collective-permute-start.1 = (bf16[128,4096]{1,0:T(8,128)(2,1)}, bf16[128,4096]{1,0:T(8,128)(2,1)S(1)}, u32[]{:S(2)}, u32[]{:S(2)}) collective-permute-start(bf16[128,4096]{1,0:T(8,128)(2,1)} %get-tuple-element.1094), channel_id=1, source_target_pairs={{8,0},{16,8},{24,16},{9,1},{17,9},{25,17},{10,2},{18,10},{26,18},{... | collective-permute-start | bytes 3145736 | tf_op jit(solution)/shard_map/while/body/eval_jaxpr/ppermute | solution.py:12
  927.7 7.1 copy-start.6
  937.9 16.0 %copy-start.15 = (bf16[2,8,4096]{2,0,1:T(2,128)(2,1)S(1)}, bf16[2,8,4096]{2,0,1:T(2,128)(2,1)}, u32[]{:S(2)}) copy-start(bf16[2,8,4096]{2,0,1:T(2,128)(2,1)} %get-tuple-element.856) | copy-start | bytes 393220 | tf_op jit(solution)/shard_map/cond
  962.5 131.0 %reduce-scatter.3.cloned.1.call-start = ((), (), s32[]{:S(2)}) async-start(), calls=%async_computation.2 | async-start | bytes 1179648 | tf_op jit(solution)/shard_map/reduce_scatter | solution.py:172
  969.1 126.0 %copy-start.1 = (bf16[1,16,8,4096]{3,2,1,0:T(8,128)(2,1)S(1)}, bf16[1,16,8,4096]{3,2,1,0:T(8,128)(2,1)}, u32[]{:S(2)}) copy-start(bf16[1,16,8,4096]{3,2,1,0:T(8,128)(2,1)} %param.24) | copy-start | bytes 3145732
  (28 other events, 64.9 us)
Sparse Core Ops, SparseCore 0:
  9.5 640.3 all-gather.2
  962.6 63.6 reduce-scatter.4
  1029.8 63.6 reduce-scatter.2
where the time goes:
time: 1100 us
  waiting for transfers between devices  849 us (77%)
  matrix products  75.6 us (7%)
  other arithmetic  66.7 us (6%)
  starting transfers between devices  53.3 us (5%)
  local copies, waits for them, and re-layouts  42.4 us (4%)
  between operations  14 us (1%)
    all_gather x1, waiting for transfers between devices, shards(): weight = lax.all_gather(base_weight[0], 'dp', axis=0, tiled=True)  634 us
    ppermute x8, waiting for transfers between devices, shifted(): return lax.ppermute(block, axis, route)  94.9 us
    reduce_scatter x1, waiting for transfers between devices, shards(): lax.psum_scatter(acc_down.astype(jnp.bfloat16), 'dp', scatter_dimension=2...  65.5 us
    reduce_scatter x1, waiting for transfers between devices, shards(): lax.psum_scatter(acc_up.astype(jnp.bfloat16), 'dp', scatter_dimension=2,...  53.5 us
    ppermute x8, starting transfers between devices, shifted(): return lax.ppermute(block, axis, route)  53.2 us
    select_n x14, other arithmetic, place(): jnp.where(active, lax.dynamic_update_index_in_dim(table, value, index, 0)...  34.3 us
    dot_general x2, matrix products, backward_core(): dnorm = jnp.dot(grad_out, weight.T, preferred_element_type=jnp.float32)  32 us
    dot_general x2, matrix products, forward_full(): jnp.dot(normed, weight, preferred_element_type=jnp.float32)  25.9 us
  transfers between devices with their start and end apart: 11, of which 7 were waited for; matrix products, arithmetic and copies ran while one was open for 5% of the time, Pallas kernels for 0%

commit v1 on v0

--- a/solution.py
+++ b/solution.py
@@ -65,7 +65,12 @@
     segments = lax.axis_size("segment")
     segment = lax.axis_index("segment")
     member = lax.axis_index("dp")
-    weight = lax.all_gather(base_weight[0], "dp", axis=0, tiled=True)
+    ring = [base_weight[0]]
+    for hop in range(7):
+        ring.append(lax.ppermute(ring[-1], "dp", [(dev, (dev + 1) % 8) for dev in range(8)]))
+    weight = jnp.roll(
+        jnp.concatenate(ring[::-1], axis=0), (lax.axis_index("dp") + 1) * ring[0].shape[0], axis=0
+    )
     gain = norm_gain[0]
     micro = embeds.shape[0]
     rows = embeds.shape[2]

time: 1100 us -> 1200 us (1.091)
  local copies, waits for them, and re-layouts: 42.4 us -> 135 us
    ppermute x0 -> x7, waiting for transfers between devices: none -> 637 us  [shards(): lax.ppermute(ring[-1], 'dp', [(dev, (dev + 1) % 8) for dev in range(8)])]
    all_gather x1 -> x0, waiting for transfers between devices: 634 us -> none  [shards(): weight = lax.all_gather(base_weight[0], 'dp', axis=0, tiled=True)]
    unnamed x32 -> x65, local copies, waits for them, and re-layouts: 4.84 us -> 65.9 us
    dynamic_slice x0 -> x1, local copies, waits for them, and re-layouts: none -> 22.9 us  [shards(): jnp.roll(jnp.concatenate(ring[::-1], axis=0), (lax.axis_index('dp') + 1)...]
  transfers between devices with their start and end apart: 11 -> 17, of which waited for: 7 -> 13; matrix products, arithmetic and copies ran while one was open for 5% -> 5% of each run, Pallas kernels for 0% -> 0%
where the time goes in v1:
time: 1200 us
  waiting for transfers between devices  848 us (71%)
  local copies, waits for them, and re-layouts  135 us (11%)
  matrix products  75.4 us (6%)
  other arithmetic  69.4 us (6%)
  starting transfers between devices  54.7 us (5%)
  between operations  14.2 us (1%)
    ppermute x7, waiting for transfers between devices, shards(): lax.ppermute(ring[-1], 'dp', [(dev, (dev + 1) % 8) for dev in range(8)])  637 us
    ppermute x8, waiting for transfers between devices, shifted(): return lax.ppermute(block, axis, route)  94.9 us
    unnamed x65, local copies, waits for them, and re-layouts  65.9 us
    reduce_scatter x1, waiting for transfers between devices, shards(): lax.psum_scatter(acc_down.astype(jnp.bfloat16), 'dp', scatter_dimension=2...  65.5 us
    ppermute x8, starting transfers between devices, shifted(): return lax.ppermute(block, axis, route)  51.5 us
    reduce_scatter x1, waiting for transfers between devices, shards(): lax.psum_scatter(acc_up.astype(jnp.bfloat16), 'dp', scatter_dimension=2,...  49.9 us
    select_n x14, other arithmetic, place(): jnp.where(active, lax.dynamic_update_index_in_dim(table, value, index, 0)...  34.8 us
    dot_general x2, matrix products, backward_core(): dnorm = jnp.dot(grad_out, weight.T, preferred_element_type=jnp.float32)  32 us
  transfers between devices with their start and end apart: 17, of which 13 were waited for; matrix products, arithmetic and copies ran while one was open for 5% of the time, Pallas kernels for 0%

profile of v1, /device:TPU:0, one launch (start us, length us, event | category | flops | bytes accessed | tf_op | source)
XLA Modules:
  0.0 1197.9 jit_solution(15139325679225208291)
XLA Ops:
  10.3 93.8 %collective-permute-done.2 = bf16[512,4096]{1,0:T(8,128)(2,1)S(1)} collective-permute-done((bf16[512,4096]{1,0:T(8,128)(2,1)}, bf16[512,4096]{1,0:T(8,128)(2,1)S(1)}, u32[]{:S(2)}, u32[]{:S(2)}) %collective-permute-start.2) | collective-permute-done | bytes 4194336 | tf_op jit(solution)/shard_map/ppermute | solution.py:70
  106.2 94.4 %collective-permute-done.3 = bf16[512,4096]{1,0:T(8,128)(2,1)S(1)} collective-permute-done((bf16[512,4096]{1,0:T(8,128)(2,1)S(1)}, bf16[512,4096]{1,0:T(8,128)(2,1)S(1)}, u32[]{:S(2)}, u32[]{:S(2)}) %collective-permute-start.3) | collective-permute-done | bytes 4194336 | tf_op jit(solution)/shard_map/ppermute | solution.py:70
  202.6 93.6 %collective-permute-done.4 = bf16[512,4096]{1,0:T(8,128)(2,1)S(1)} collective-permute-done((bf16[512,4096]{1,0:T(8,128)(2,1)S(1)}, bf16[512,4096]{1,0:T(8,128)(2,1)S(1)}, u32[]{:S(2)}, u32[]{:S(2)}) %collective-permute-start.4) | collective-permute-done | bytes 4194336 | tf_op jit(solution)/shard_map/ppermute | solution.py:70
  298.1 92.7 %collective-permute-done.5 = bf16[512,4096]{1,0:T(8,128)(2,1)S(1)} collective-permute-done((bf16[512,4096]{1,0:T(8,128)(2,1)S(1)}, bf16[512,4096]{1,0:T(8,128)(2,1)S(1)}, u32[]{:S(2)}, u32[]{:S(2)}) %collective-permute-start.5) | collective-permute-done | bytes 4194336 | tf_op jit(solution)/shard_map/ppermute | solution.py:70
  392.8 91.9 %collective-permute-done.6 = bf16[512,4096]{1,0:T(8,128)(2,1)S(1)} collective-permute-done((bf16[512,4096]{1,0:T(8,128)(2,1)S(1)}, bf16[512,4096]{1,0:T(8,128)(2,1)S(1)}, u32[]{:S(2)}, u32[]{:S(2)}) %collective-permute-start.6) | collective-permute-done | bytes 4194336 | tf_op jit(solution)/shard_map/ppermute | solution.py:70
  486.7 91.1 %collective-permute-done.7 = bf16[512,4096]{1,0:T(8,128)(2,1)} collective-permute-done((bf16[512,4096]{1,0:T(8,128)(2,1)S(1)}, bf16[512,4096]{1,0:T(8,128)(2,1)}, u32[]{:S(2)}, u32[]{:S(2)}) %collective-permute-start.7) | collective-permute-done | bytes 4194336 | tf_op jit(solution)/shard_map/ppermute | solution.py:70
  588.7 79.6 %collective-permute-done.8 = bf16[512,4096]{1,0:T(8,128)(2,1)} collective-permute-done((bf16[512,4096]{1,0:T(8,128)(2,1)}, bf16[512,4096]{1,0:T(8,128)(2,1)}, u32[]{:S(2)}, u32[]{:S(2)}) %collective-permute-start.8) | collective-permute-done | bytes 4194336 | tf_op jit(solution)/shard_map/ppermute | solution.py:70
  721.6 22.9 %constant_dynamic-slice_fusion.4 = bf16[4096,4096]{1,0:T(8,128)(2,1)} fusion(bf16[8192,4096]{1,0:T(8,128)(2,1)} %constant_dynamic-update-slice_fusion, s32[]{:T(128)S(6)} %select_n.179), kind=kLoop, calls=%fused_computation.176 | loop fusion | bytes 67108864 | tf_op jit(solution)/shard_map/jit(_roll_dynamic)/dynamic_slice | solution.py:71
  747.4 115.8 %while.40 = (s32[]{:T(128)}, bf16[128,4096]{1,0:T(8,128)(2,1)}, bf16[2,128,4096]{2,1,0:T(8,128)(2,1)S(1)}, bf16[2,128,4096]{2,1,0:T(8,128)(2,1)}, s32[]{:T(128)}...) while((s32[]{:T(128)}, bf16[128,4096]{1,0:T(8,128)(2,1)}, ...), condition=%wide.region_5.6_spmd, body=%wide.region_1.5_spmd.sunk | while | flops 4321182720 | bytes 77762976 | solution.py:134
  750.6 18.8 %conditional.9 = (bf16[128,4096]{1,0:T(8,128)(2,1)}, bf16[1,128,4096]{2,1,0:T(8,128)(2,1)}) conditional(s32[]{:T(128)} %convert_element_type.342, () %tuple.144, (bf16[128,4096]{1,0:T(8,128)(2,1)S(1)}, f32[1,4096]{1,0:T(1,128)S(1)}, bf16[4096,4096]{1,0:T(8,128)(2,1)}, s32[]{:T(128)}, bf16[2,8,4096]{2,1,0:T(8,128)(2,1)S(1)}, ...), branch_computations={%region_2.2_spmd, %region_3.4_spmd} | conditional | flops 4319609856 | bytes 44207664 | solution.py:114
  750.9 13.0 %convolution_add_fusion.1 = f32[128,4096]{1,0:T(8,128)S(1)} fusion(bf16[4096,4096]{1,0:T(8,128)(2,1)} %get-tuple-element.684, bf16[128,4096]{1,0:T(8,128)(2,1)S(1)} %get-tuple-element.682, f32[4096]{0:T(1024)S(1)} %bitcast.181, f32[128]{0:T(128)S(1)} %add_rsqrt_fusion), kind=kOutput, calls=%fused_computation.1 | convolution fusion | flops 4298113024 | bytes 36717056 | tf_op jit(solution)/shard_map/while/body/eval_jaxpr/cond/branch_1_fun/dot_general | solution.py:25
  777.8 18.8 %conditional.9 = (bf16[128,4096]{1,0:T(8,128)(2,1)}, bf16[1,128,4096]{2,1,0:T(8,128)(2,1)}) conditional(s32[]{:T(128)} %convert_element_type.342, () %tuple.144, (bf16[128,4096]{1,0:T(8,128)(2,1)S(1)}, f32[1,4096]{1,0:T(1,128)S(1)}, bf16[4096,4096]{1,0:T(8,128)(2,1)}, s32[]{:T(128)}, bf16[2,8,4096]{2,1,0:T(8,128)(2,1)S(1)}, ...), branch_computations={%region_2.2_spmd, %region_3.4_spmd} | conditional | flops 4319609856 | bytes 44207664 | solution.py:114
  778.1 13.0 %convolution_add_fusion.1 = f32[128,4096]{1,0:T(8,128)S(1)} fusion(bf16[4096,4096]{1,0:T(8,128)(2,1)} %get-tuple-element.684, bf16[128,4096]{1,0:T(8,128)(2,1)S(1)} %get-tuple-element.682, f32[4096]{0:T(1024)S(1)} %bitcast.181, f32[128]{0:T(128)S(1)} %add_rsqrt_fusion), kind=kOutput, calls=%fused_computation.1 | convolution fusion | flops 4298113024 | bytes 36717056 | tf_op jit(solution)/shard_map/while/body/eval_jaxpr/cond/branch_1_fun/dot_general | solution.py:25
  808.3 28.2 %collective-permute-start = (bf16[128,4096]{1,0:T(8,128)(2,1)}, bf16[128,4096]{1,0:T(8,128)(2,1)S(1)}, u32[]{:S(2)}, u32[]{:S(2)}) collective-permute-start(bf16[128,4096]{1,0:T(8,128)(2,1)} %get-tuple-element.1077), channel_id=1, source_target_pairs={{0,8},{8,16},{16,24},{1,9},{9,17},{17,25},{2,10},{10,18},{18,26},{... | collective-permute-start | bytes 3145736 | tf_op jit(solution)/shard_map/while/body/eval_jaxpr/ppermute | solution.py:12
  845.4 14.3 %collective-permute-start = (bf16[128,4096]{1,0:T(8,128)(2,1)}, bf16[128,4096]{1,0:T(8,128)(2,1)S(1)}, u32[]{:S(2)}, u32[]{:S(2)}) collective-permute-start(bf16[128,4096]{1,0:T(8,128)(2,1)} %get-tuple-element.1077), channel_id=1, source_target_pairs={{0,8},{8,16},{16,24},{1,9},{9,17},{17,25},{2,10},{10,18},{18,26},{... | collective-permute-start | bytes 3145736 | tf_op jit(solution)/shard_map/while/body/eval_jaxpr/ppermute | solution.py:12
  868.7 166.1 %while.41 = (s32[]{:T(128)}, bf16[128,4096]{1,0:T(8,128)(2,1)}, bf16[2,128,4096]{2,1,0:T(8,128)(2,1)}, f32[16,8,4096]{2,1,0:T(8,128)}, f32[16,8,4096]{2,1,0:T(8,...) while((s32[]{:T(128)}, bf16[128,4096]{1,0:T(8,128)(2,1)}, ...), condition=%wide.region_14.15_spmd.clone, body=%wide.region_9.14_spmd.clone.sunk | while | flops 4354214400 | bytes 94118616 | solution.py:174
  878.3 25.7 %collective-permute-done.1 = bf16[128,4096]{1,0:T(8,128)(2,1)S(1)} collective-permute-done((bf16[128,4096]{1,0:T(8,128)(2,1)}, bf16[128,4096]{1,0:T(8,128)(2,1)S(1)}, u32[]{:S(2)}, u32[]{:S(2)}) %collective-permute-start.1) | collective-permute-done | bytes 1048608 | tf_op jit(solution)/shard_map/while/body/eval_jaxpr/ppermute | solution.py:12
  936.5 54.0 %collective-permute-done.1 = bf16[128,4096]{1,0:T(8,128)(2,1)S(1)} collective-permute-done((bf16[128,4096]{1,0:T(8,128)(2,1)}, bf16[128,4096]{1,0:T(8,128)(2,1)S(1)}, u32[]{:S(2)}, u32[]{:S(2)}) %collective-permute-start.1) | collective-permute-done | bytes 1048608 | tf_op jit(solution)/shard_map/while/body/eval_jaxpr/ppermute | solution.py:12
  991.5 26.0 %conditional.10 = (bf16[128,4096]{1,0:T(8,128)(2,1)}, f32[8,4096]{1,0:T(8,128)S(1)}, f32[8,4096]{1,0:T(8,128)S(1)}, bf16[1,128,4096]{2,1,0:T(8,128)(2,1)}) conditional(s32[]{:T(128)} %convert_element_type.343, () %tuple.148, (pred[]{:T(512)}, bf16[2,128,4096]{2,1,0:T(8,128)(2,1)}, s32[]{:T(128)}, bf16[128,4096]{1,0:T(8,128)(2,1)}, ...), branch_computations={%region_10.10_spmd, %region_11.13_spmd} | conditional | flops 4350544384 | bytes 57155172 | solution.py:153
  994.4 16.0 %fusion.153 = f32[128,4096]{1,0:T(8,128)S(1)} fusion(bf16[128,4096]{1,0:T(8,128)(2,1)S(1)} %bitcast_select_fusion.2, bf16[4096,4096]{1,0:T(8,128)(2,1)} %get-tuple-element.714), kind=kOutput, calls=%fused_computation.183 | convolution fusion | flops 4294967296 | bytes 36700160 | tf_op jit(solution)/shard_map/while/body/eval_jaxpr/cond/branch_1_fun/dot_general | solution.py:32
  1034.8 22.6 %conditional.5 = (f32[8,4096]{1,0:T(8,128)S(1)}, f32[8,4096]{1,0:T(8,128)S(1)}, bf16[1,128,4096]{2,1,0:T(8,128)(2,1)}) conditional(s32[]{:T(128)} %convert_element_type.170, () %tuple.98, (pred[]{:T(512)}, bf16[2,128,4096]{2,1,0:T(8,128)(2,1)}, s32[]{:T(128)}, bf16[128,4096]{1,0:T(8,128)(2,1)}, bf16[2,8,4096]{2,0,1:T(2,128)(2,1)}, ...), branch_computations={%region_15.16_spmd, %region_16.19_spmd} | conditional | flops 4350544384 | bytes 56620128 | solution.py:153
  1037.0 16.0 %fusion.154 = f32[128,4096]{1,0:T(8,128)S(1)} fusion(bf16[128,4096]{1,0:T(8,128)(2,1)S(1)} %bitcast_select_fusion.3, bf16[4096,4096]{1,0:T(8,128)(2,1)} %get-tuple-element.744), kind=kOutput, calls=%fused_computation.184 | convolution fusion | flops 4294967296 | bytes 36700160 | tf_op jit(solution)/shard_map/cond/branch_1_fun/dot_general | solution.py:32
  1072.4 49.9 %reduce-scatter.5.cloned.1.call-done = bf16[16,8,512]{2,1,0:T(8,128)(2,1)} async-done(((bf16[16,8,4096]{2,1,0:T(8,128)(2,1)}), bf16[16,8,512]{2,1,0:T(8,128)(2,1)}) %reduce-scatter.5.cloned.1.call-update) | async-done | bytes 131088 | tf_op jit(solution)/shard_map/reduce_scatter | solution.py:180
  1123.9 65.5 %reduce-scatter.3.cloned.1.call-done = bf16[16,8,512]{2,1,0:T(8,128)(2,1)} async-done(((bf16[16,8,4096]{2,1,0:T(8,128)(2,1)}), bf16[16,8,512]{2,1,0:T(8,128)(2,1)}) %reduce-scatter.3.cloned.1.call-update) | async-done | bytes 131088 | tf_op jit(solution)/shard_map/reduce_scatter | solution.py:177
  (237 shorter events, 240.0 us)
Async XLA Ops:
  7.2 573.6 %copy-start = (bf16[1,16,8,4096]{3,2,1,0:T(8,128)(2,1)S(1)}, bf16[1,16,8,4096]{3,2,1,0:T(8,128)(2,1)}, u32[]{:S(2)}) copy-start(bf16[1,16,8,4096]{3,2,1,0:T(8,128)(2,1)} %param.24) | copy-start | bytes 3145732
  7.2 575.3 %copy-start.29 = (bf16[1,16,8,4096]{3,2,1,0:T(8,128)(2,1)S(1)}, bf16[1,16,8,4096]{3,2,1,0:T(8,128)(2,1)}, u32[]{:S(2)}) copy-start(bf16[1,16,8,4096]{3,2,1,0:T(8,128)(2,1)} %param.25) | copy-start | bytes 3145732
  7.2 577.6 %copy-start.34 = (s32[2,8]{1,0:T(2,128)S(1)}, s32[2,8]{1,0:T(2,128)}, u32[]{:S(2)}) copy-start(s32[2,8]{1,0:T(2,128)} %param.28) | copy-start | bytes 196
  7.2 1115.1 %reduce-scatter.5.cloned.1.call-start = ((), (), s32[]{:S(2)}) async-start(), calls=%async_computation.3 | async-start | bytes 1179648 | tf_op jit(solution)/shard_map/reduce_scatter | solution.py:180
  7.2 96.9 %collective-permute-start.2 = (bf16[512,4096]{1,0:T(8,128)(2,1)}, bf16[512,4096]{1,0:T(8,128)(2,1)S(1)}, u32[]{:S(2)}, u32[]{:S(2)}) collective-permute-start(bf16[512,4096]{1,0:T(8,128)(2,1)} %bitcast.180), channel_id=1, source_target_pairs={{0,1},{1,2},{2,3},{3,4},{4,5},{5,6},{6,7},{7,0},{8,9},{9,10},{10,1... | collective-permute-start | bytes 12582920 | tf_op jit(solution)/shard_map/ppermute | solution.py:70
  106.1 94.4 %collective-permute-start.3 = (bf16[512,4096]{1,0:T(8,128)(2,1)S(1)}, bf16[512,4096]{1,0:T(8,128)(2,1)S(1)}, u32[]{:S(2)}, u32[]{:S(2)}) collective-permute-start(bf16[512,4096]{1,0:T(8,128)(2,1)S(1)} %collective-permute-done.2), channel_id=1, source_target_pairs={{0,1},{1,2},{2,3},{3,4},{4,5},{5,6},{6,7},{7,0},{8,9},{9,10},{10,1... | collective-permute-start | bytes 12582920 | tf_op jit(solution)/shard_map/ppermute | solution.py:70
  202.6 93.6 %collective-permute-start.4 = (bf16[512,4096]{1,0:T(8,128)(2,1)S(1)}, bf16[512,4096]{1,0:T(8,128)(2,1)S(1)}, u32[]{:S(2)}, u32[]{:S(2)}) collective-permute-start(bf16[512,4096]{1,0:T(8,128)(2,1)S(1)} %collective-permute-done.3), channel_id=1, source_target_pairs={{0,1},{1,2},{2,3},{3,4},{4,5},{5,6},{6,7},{7,0},{8,9},{9,10},{10,1... | collective-permute-start | bytes 12582920 | tf_op jit(solution)/shard_map/ppermute | solution.py:70
  298.1 92.7 %collective-permute-start.5 = (bf16[512,4096]{1,0:T(8,128)(2,1)S(1)}, bf16[512,4096]{1,0:T(8,128)(2,1)S(1)}, u32[]{:S(2)}, u32[]{:S(2)}) collective-permute-start(bf16[512,4096]{1,0:T(8,128)(2,1)S(1)} %collective-permute-done.4), channel_id=1, source_target_pairs={{0,1},{1,2},{2,3},{3,4},{4,5},{5,6},{6,7},{7,0},{8,9},{9,10},{10,1... | collective-permute-start | bytes 12582920 | tf_op jit(solution)/shard_map/ppermute | solution.py:70
  392.8 91.9 %collective-permute-start.6 = (bf16[512,4096]{1,0:T(8,128)(2,1)S(1)}, bf16[512,4096]{1,0:T(8,128)(2,1)S(1)}, u32[]{:S(2)}, u32[]{:S(2)}) collective-permute-start(bf16[512,4096]{1,0:T(8,128)(2,1)S(1)} %collective-permute-done.5), channel_id=1, source_target_pairs={{0,1},{1,2},{2,3},{3,4},{4,5},{5,6},{6,7},{7,0},{8,9},{9,10},{10,1... | collective-permute-start | bytes 12582920 | tf_op jit(solution)/shard_map/ppermute | solution.py:70
  486.7 91.1 %collective-permute-start.7 = (bf16[512,4096]{1,0:T(8,128)(2,1)S(1)}, bf16[512,4096]{1,0:T(8,128)(2,1)}, u32[]{:S(2)}, u32[]{:S(2)}) collective-permute-start(bf16[512,4096]{1,0:T(8,128)(2,1)S(1)} %collective-permute-done.6), channel_id=1, source_target_pairs={{0,1},{1,2},{2,3},{3,4},{4,5},{5,6},{6,7},{7,0},{8,9},{9,10},{10,1... | collective-permute-start | bytes 12582920 | tf_op jit(solution)/shard_map/ppermute | solution.py:70
  577.8 90.5 %collective-permute-start.8 = (bf16[512,4096]{1,0:T(8,128)(2,1)}, bf16[512,4096]{1,0:T(8,128)(2,1)}, u32[]{:S(2)}, u32[]{:S(2)}) collective-permute-start(bf16[512,4096]{1,0:T(8,128)(2,1)} %collective-permute-done.7), channel_id=1, source_target_pairs={{0,1},{1,2},{2,3},{3,4},{4,5},{5,6},{6,7},{7,0},{8,9},{9,10},{10,1... | collective-permute-start | bytes 12582920 | tf_op jit(solution)/shard_map/ppermute | solution.py:70
  769.4 4.3 collective-permute-start
  796.7 5.2 collective-permute-start
  808.3 31.7 %copy-start.3 = (bf16[2,128,4096]{2,1,0:T(8,128)(2,1)S(1)}, bf16[2,128,4096]{2,1,0:T(8,128)(2,1)}, u32[]{:S(2)}) copy-start(bf16[2,128,4096]{2,1,0:T(8,128)(2,1)} %copy-done.2) | copy-start | bytes 6291460 | tf_op jit(solution)/shard_map/while
  808.3 30.7 %collective-permute-start = (bf16[128,4096]{1,0:T(8,128)(2,1)}, bf16[128,4096]{1,0:T(8,128)(2,1)S(1)}, u32[]{:S(2)}, u32[]{:S(2)}) collective-permute-start(bf16[128,4096]{1,0:T(8,128)(2,1)} %get-tuple-element.1077), channel_id=1, source_target_pairs={{0,8},{8,16},{16,24},{1,9},{9,17},{17,25},{2,10},{10,18},{18,26},{... | collective-permute-start | bytes 3145736 | tf_op jit(solution)/shard_map/while/body/eval_jaxpr/ppermute | solution.py:12
  845.4 16.8 %collective-permute-start = (bf16[128,4096]{1,0:T(8,128)(2,1)}, bf16[128,4096]{1,0:T(8,128)(2,1)S(1)}, u32[]{:S(2)}, u32[]{:S(2)}) collective-permute-start(bf16[128,4096]{1,0:T(8,128)(2,1)} %get-tuple-element.1077), channel_id=1, source_target_pairs={{0,8},{8,16},{16,24},{1,9},{9,17},{17,25},{2,10},{10,18},{18,26},{... | collective-permute-start | bytes 3145736 | tf_op jit(solution)/shard_map/while/body/eval_jaxpr/ppermute | solution.py:12
  871.0 33.1 %collective-permute-start.1 = (bf16[128,4096]{1,0:T(8,128)(2,1)}, bf16[128,4096]{1,0:T(8,128)(2,1)S(1)}, u32[]{:S(2)}, u32[]{:S(2)}) collective-permute-start(bf16[128,4096]{1,0:T(8,128)(2,1)} %get-tuple-element.1094), channel_id=1, source_target_pairs={{8,0},{16,8},{24,16},{9,1},{17,9},{25,17},{10,2},{18,10},{26,18},{... | collective-permute-start | bytes 3145736 | tf_op jit(solution)/shard_map/while/body/eval_jaxpr/ppermute | solution.py:12
  878.3 25.7 %copy-start.5 = (f32[16,8,4096]{2,1,0:T(8,128)}, f32[16,8,4096]{2,1,0:T(8,128)S(1)}, u32[]{:S(2)}) copy-start(f32[16,8,4096]{2,1,0:T(8,128)S(1)} %get-tuple-element.1191) | copy-start | bytes 6291460 | tf_op jit(solution)/shard_map/while
  907.3 17.0 %collective-permute-start.1 = (bf16[128,4096]{1,0:T(8,128)(2,1)}, bf16[128,4096]{1,0:T(8,128)(2,1)S(1)}, u32[]{:S(2)}, u32[]{:S(2)}) collective-permute-start(bf16[128,4096]{1,0:T(8,128)(2,1)} %get-tuple-element.1094), channel_id=1, source_target_pairs={{8,0},{16,8},{24,16},{9,1},{17,9},{25,17},{10,2},{18,10},{26,18},{... | collective-permute-start | bytes 3145736 | tf_op jit(solution)/shard_map/while/body/eval_jaxpr/ppermute | solution.py:12
  927.6 62.9 %collective-permute-start.1 = (bf16[128,4096]{1,0:T(8,128)(2,1)}, bf16[128,4096]{1,0:T(8,128)(2,1)S(1)}, u32[]{:S(2)}, u32[]{:S(2)}) collective-permute-start(bf16[128,4096]{1,0:T(8,128)(2,1)} %get-tuple-element.1094), channel_id=1, source_target_pairs={{8,0},{16,8},{24,16},{9,1},{17,9},{25,17},{10,2},{18,10},{26,18},{... | collective-permute-start | bytes 3145736 | tf_op jit(solution)/shard_map/while/body/eval_jaxpr/ppermute | solution.py:12
  936.5 54.0 %copy-start.5 = (f32[16,8,4096]{2,1,0:T(8,128)}, f32[16,8,4096]{2,1,0:T(8,128)S(1)}, u32[]{:S(2)}) copy-start(f32[16,8,4096]{2,1,0:T(8,128)S(1)} %get-tuple-element.1191) | copy-start | bytes 6291460 | tf_op jit(solution)/shard_map/while
  1017.5 16.3 %collective-permute-start.1 = (bf16[128,4096]{1,0:T(8,128)(2,1)}, bf16[128,4096]{1,0:T(8,128)(2,1)S(1)}, u32[]{:S(2)}, u32[]{:S(2)}) collective-permute-start(bf16[128,4096]{1,0:T(8,128)(2,1)} %get-tuple-element.1094), channel_id=1, source_target_pairs={{8,0},{16,8},{24,16},{9,1},{17,9},{25,17},{10,2},{18,10},{26,18},{... | collective-permute-start | bytes 3145736 | tf_op jit(solution)/shard_map/while/body/eval_jaxpr/ppermute | solution.py:12
  1061.6 127.8 %reduce-scatter.3.cloned.1.call-start = ((), (), s32[]{:S(2)}) async-start(), calls=%async_computation.2 | async-start | bytes 1179648 | tf_op jit(solution)/shard_map/reduce_scatter | solution.py:177
  1068.3 122.8 %copy-start.1 = (bf16[1,16,8,4096]{3,2,1,0:T(8,128)(2,1)S(1)}, bf16[1,16,8,4096]{3,2,1,0:T(8,128)(2,1)}, u32[]{:S(2)}) copy-start(bf16[1,16,8,4096]{3,2,1,0:T(8,128)(2,1)} %param.24) | copy-start | bytes 3145732
  (45 other events, 176.3 us)
Sparse Core Ops, SparseCore 0:
  1061.7 60.5 reduce-scatter.4
  1125.7 63.7 reduce-scatter.2
